TPU v7x, 32 devices: a whole 2x2x4 slice. The times are simulated.
32 devices in a mesh: row: 8 (over y, x, core), col: 4 (over z).
Axes of the slice: x: 2, y: 2, z: 4, core: 2. Of those that a mesh axis runs over, the one named last changes fastest.
Arguments:
- field: float32 [64, 128, 512], P(None, 'row', 'col'), may hold values from -4 to 6.5, as said below
- conductivity: float32 [64, 128, 512], P(None, 'row', 'col'), may hold values from 35 to 5600, as said below
Outputs:
- new_field: float32 [64, 128, 512], P(None, 'row', 'col')
Inputs may be any that keep to these rules, and one draw needn't show every extreme that they name: `field`: finite values. `conductivity`: positive in every cell.
All inputs are finite; a program needn't handle non-finite values.
Results may differ from a plain program's by a relative error of at most 0.0003.
Values sent between devices are 32-bit elements; how exact they have to be, the bound alone decides.
A program may use at most 64 MiB of HBM per device.

v0:
```python
import jax
import jax.numpy as jnp
from jax import lax
from jax.sharding import PartitionSpec as P

z_weight = 0.02


def padded_2(block, sides, width):
    for axis, dim in sides:
        count = lax.axis_size(axis)
        forward = [(i, i + 1) for i in range(count - 1)]
        backward = [(target, source) for source, target in forward]
        low = lax.ppermute(
            lax.slice_in_dim(block, block.shape[dim] - width, None, axis=dim), axis, forward
        )
        high = lax.ppermute(lax.slice_in_dim(block, 0, width, axis=dim), axis, backward)
        block = jnp.concatenate([low, block, high], axis=dim)
    return block


def neighbour(values, line_axis, offset):
    length = values.shape[line_axis]
    widths = [(0, 0)] * values.ndim
    widths[line_axis] = (1, 1)
    padded = jnp.pad(values, widths)
    return lax.slice_in_dim(padded, 1 + offset, 1 + offset + length, axis=line_axis)


def shifted(values, line_axis, stride, fill):
    length = values.shape[line_axis]
    pad_shape = list(values.shape)
    pad_shape[line_axis] = abs(stride)
    padding = jnp.full(pad_shape, fill, values.dtype)
    if stride > 0:
        kept_part = lax.slice_in_dim(values, 0, length - stride, axis=line_axis)
        return jnp.concatenate((padding, kept_part), axis=line_axis)
    kept_part = lax.slice_in_dim(values, -stride, length, axis=line_axis)
    return jnp.concatenate((kept_part, padding), axis=line_axis)


def reduce_lines(below_diag, diagonal, above_diag, columns, line_axis):
    length = diagonal.shape[line_axis]
    stride = 1
    while stride < length:
        left_factor = -below_diag / shifted(diagonal, line_axis, stride, 1.0)
        right_factor = -above_diag / shifted(diagonal, line_axis, -stride, 1.0)
        new_diag = (
            diagonal
            + left_factor * shifted(above_diag, line_axis, stride, 0.0)
            + right_factor * shifted(below_diag, line_axis, -stride, 0.0)
        )
        new_below = left_factor * shifted(below_diag, line_axis, stride, 0.0)
        new_above = right_factor * shifted(above_diag, line_axis, -stride, 0.0)
        columns = [
            column
            + left_factor * shifted(column, line_axis, stride, 0.0)
            + right_factor * shifted(column, line_axis, -stride, 0.0)
            for column in columns
        ]
        below_diag, diagonal, above_diag = (new_below, new_diag, new_above)
        stride = stride * 2
    return (diagonal, columns)


def local_spikes(below_diag, above_diag, right_side, line_axis):
    length = right_side.shape[line_axis]
    position = lax.broadcasted_iota(jnp.int32, right_side.shape, line_axis)
    first_row = position == 0
    last_row = position == length - 1
    diagonal = 1.0 - below_diag - above_diag
    left_column = jnp.where(first_row, below_diag, 0.0)
    right_column = jnp.where(last_row, above_diag, 0.0)
    below_inner = jnp.where(first_row, 0.0, below_diag)
    above_inner = jnp.where(last_row, 0.0, above_diag)
    diagonal, columns = reduce_lines(
        below_inner, diagonal, above_inner, [right_side, left_column, right_column], line_axis
    )
    local_part = columns[0] / diagonal
    left_spike = columns[1] / diagonal
    right_spike = columns[2] / diagonal
    planes = []
    for member in (local_part, left_spike, right_spike):
        planes.append(lax.index_in_dim(member, 0, line_axis, keepdims=False))
        planes.append(lax.index_in_dim(member, length - 1, line_axis, keepdims=False))
    return (local_part, left_spike, right_spike, jnp.stack(planes)[None])


def join_spikes(gathered, local_part, left_spike, right_spike, line_axis, index_here, group_size):
    columns_in = tuple((gathered[:, member] for member in range(6)))
    zero_plane = jnp.zeros_like(columns_in[0][0])

    def forward(state_now, inputs):
        spike_prev, carry_prev = state_now
        head_local, tail_local, head_left, tail_left, head_right, tail_right = inputs
        pivot_here = 1.0 - head_left * spike_prev
        ratio_here = head_right / pivot_here
        first_here = (head_local - head_left * carry_prev) / pivot_here
        spike_next = tail_right + tail_left * spike_prev * ratio_here
        carry_next = tail_local - tail_left * carry_prev + tail_left * spike_prev * first_here
        return ((spike_next, carry_next), (ratio_here, spike_next, first_here, carry_next))

    unused, outputs = lax.scan(forward, (zero_plane, zero_plane), columns_in)

    def backward(next_head, inputs):
        ratio_here, spike_here, first_here, last_here = inputs
        head_value = first_here - ratio_here * next_head
        tail_value = last_here - spike_here * next_head
        return (head_value, (head_value, tail_value))

    unused_last, ends = lax.scan(backward, zero_plane, outputs, reverse=True)
    first_values, last_values = ends
    left_value = lax.dynamic_index_in_dim(
        last_values, jnp.maximum(index_here - 1, 0), 0, keepdims=False
    ) * (index_here > 0).astype(jnp.float32)
    right_value = lax.dynamic_index_in_dim(
        first_values, jnp.minimum(index_here + 1, group_size - 1), 0, keepdims=False
    ) * (index_here < group_size - 1).astype(jnp.float32)
    return (
        local_part
        - jnp.expand_dims(left_value, line_axis) * left_spike
        - jnp.expand_dims(right_value, line_axis) * right_spike
    )


def on_device(field, conductivity):
    stacked = jnp.stack((field, conductivity))
    padded = padded_2(stacked, (("row", 2), ("col", 3)), 1)
    field_pad = padded[0]
    cond_pad = padded[1]
    west_cond = cond_pad[:, :-2, 1:-1]
    east_cond = cond_pad[:, 2:, 1:-1]
    south_cond = cond_pad[:, 1:-1, :-2]
    north_cond = cond_pad[:, 1:-1, 2:]
    west_field = field_pad[:, :-2, 1:-1]
    east_field = field_pad[:, 2:, 1:-1]
    south_field = field_pad[:, 1:-1, :-2]
    north_field = field_pad[:, 1:-1, 2:]
    east_xdir = 0.5 * 1.0 * (conductivity + east_cond)
    west_xdir = 0.5 * 1.0 * (conductivity + west_cond)
    east_ydir = 0.5 * 1.0 * (conductivity + north_cond)
    west_ydir = 0.5 * 1.0 * (conductivity + south_cond)
    flux_xdir = east_xdir * (east_field - field) - west_xdir * (field - west_field)
    flux_ydir = east_ydir * (north_field - field) - west_ydir * (field - south_field)
    east_zdir = 0.5 * z_weight * (conductivity + neighbour(conductivity, 0, 1))
    west_zdir = 0.5 * z_weight * (conductivity + neighbour(conductivity, 0, -1))
    flux_zdir = east_zdir * (neighbour(field, 0, 1) - field) - west_zdir * (
        field - neighbour(field, 0, -1)
    )
    explicit = flux_xdir + flux_ydir + flux_zdir
    local_part, left_spike, right_spike, planes = local_spikes(-west_xdir, -east_xdir, explicit, 1)
    gathered = lax.all_gather(planes, "row", axis=0, tiled=True)
    delta_xdir = join_spikes(
        gathered,
        local_part,
        left_spike,
        right_spike,
        1,
        lax.axis_index("row"),
        lax.axis_size("row"),
    )
    local_part, left_spike, right_spike, planes = local_spikes(
        -west_ydir, -east_ydir, delta_xdir, 2
    )
    gathered = lax.all_gather(planes, "col", axis=0, tiled=True)
    delta_ydir = join_spikes(
        gathered,
        local_part,
        left_spike,
        right_spike,
        2,
        lax.axis_index("col"),
        lax.axis_size("col"),
    )
    return field + delta_ydir


def solution(mesh):
    in_specs = (P(None, "row", "col"), P(None, "row", "col"))
    out_specs = P(None, "row", "col")
    return jax.shard_map(
        on_device, mesh=mesh, in_specs=in_specs, out_specs=out_specs, check_vma=False
    )
```

profile of v0, /device:TPU:0, one launch (start us, length us, event | category | flops | bytes accessed | tf_op | source)
XLA Modules:
  0.0 144.2 jit_solution(15308119017377806291)
XLA Ops:
  6.5 2.5 %fusion.59 = (f32[64,16,128]{2,0,1:T(8,128)}, f32[1,64,16,128]{3,1,2,0:T(8,128)S(1)}, f32[1,64,16,128]{3,1,2,0:T(8,128)S(1)}, f32[64,16,128]{2,0,1:T(8,128)}) fusion(f32[64,16,128]{2,1,0:T(8,128)} %param.10, f32[64,16,128]{2,1,0:T(8,128)} %param.11), kind=kLoop, calls=%fused_computation.241 | loop fusion | bytes 3145728 | tf_op args[0]
  10.4 3.0 %collective-permute-start = (f32[2,64,1,128]{3,1,2,0:T(8,128)S(1)}, f32[2,64,1,128]{3,1,2,0:T(8,128)S(1)}, u32[]{:S(2)}, u32[]{:S(2)}) collective-permute-start(f32[2,64,1,128]{3,1,2,0:T(8,128)S(1)} %get-tuple-element.850), channel_id=1, source_target_pairs={{0,4},{4,8},{8,12},{12,16},{16,20},{20,24},{24,28},{1,5},{5,9},{9,... | collective-permute-start | bytes 196616 | tf_op jit(solution)/shard_map/ppermute | solution.py:14
  17.6 6.2 %collective-permute-start.2 = (f32[2,64,18,1]{1,0,3,2:T(2,128)S(1)}, f32[2,64,18,1]{1,0,3,2:T(2,128)}, u32[]{:S(2)}, u32[]{:S(2)}) collective-permute-start(f32[2,64,18,1]{1,0,3,2:T(2,128)S(1)} %copy.303), channel_id=1, source_target_pairs={{0,1},{1,2},{2,3},{4,5},{5,6},{6,7},{8,9},{9,10},{10,11},{12,13},{... | collective-permute-start | bytes 27656 | tf_op jit(solution)/shard_map/ppermute | solution.py:14
  45.8 23.3 %all-gather.4.cloned.1.call-done = f32[48,64,128]{2,1,0:T(8,128)} async-done(((f32[6,64,128]{2,1,0:T(8,128)}), f32[48,64,128]{2,1,0:T(8,128)}) %all-gather.4.cloned.1.call-update) | async-done | bytes 1572880 | tf_op jit(solution)/shard_map/all_gather | solution.py:152
  69.1 2.4 %slice_bitcast_fusion.2 = (f32[8,64,128]{2,1,0:T(8,128)S(1)}, f32[8,64,128]{2,1,0:T(8,128)S(1)}, f32[8,64,128]{2,1,0:T(8,128)}, f32[8,64,128]{2,1,0:T(8,128)}, f32[8,64,128]{2,1,0:T(8,128)}, /*index=5*/f32[8,64,128]{2,1,0:T(8,128)}) fusion(f32[8,6,64,128]{3,2,1,0:T(8,128)} %bitcast.281), kind=kLoop, calls=%fused_computation.177 | loop fusion | bytes 3145728 | tf_op jit(solution)/shard_map/squeeze | solution.py:90
  74.4 12.1 %while.80 = (s32[]{:T(128)}, f32[64,128]{1,0:T(8,128)S(1)}, f32[64,128]{1,0:T(8,128)S(1)}, f32[8,64,128]{2,1,0:T(8,128)}, f32[8,64,128]{2,1,0:T(8,128)}, /*index...) while((s32[]{:T(128)}, f32[64,128]{1,0:T(8,128)S(1)}, ...), condition=%wide.region_1.2_spmd.clone, body=%wide.region_0.1_spmd.clone.sunk | while | flops 122883 | bytes 458915 | solution.py:103
  74.4 1.6 %bitcast_dynamic-update-slice_fusion.16 = (f32[8,64,128]{2,1,0:T(8,128)}, f32[64,128]{1,0:T(8,128)S(1)}, f32[8,64,128]{2,1,0:T(8,128)}, f32[8,64,128]{2,1,0:T(8,...) fusion(f32[8,64,128]{2,1,0:T(8,128)} %get-tuple-element.1309, s32[]{:T(128)S(6)} %copy.408, ...), kind=kLoop, calls=%fused_computation.clone.1 | loop fusion | flops 122880 | bytes 458757 | tf_op jit(solution)/shard_map/while/body/jit(dynamic_update_index_in_dim)/dynamic_update_slice | solution.py:103
  76.0 1.5 %bitcast_dynamic-update-slice_fusion.16 = (f32[8,64,128]{2,1,0:T(8,128)}, f32[64,128]{1,0:T(8,128)S(1)}, f32[8,64,128]{2,1,0:T(8,128)}, f32[8,64,128]{2,1,0:T(8,...) fusion(f32[8,64,128]{2,1,0:T(8,128)} %get-tuple-element.1309, s32[]{:T(128)S(6)} %copy.408, ...), kind=kLoop, calls=%fused_computation.clone.1 | loop fusion | flops 122880 | bytes 458757 | tf_op jit(solution)/shard_map/while/body/jit(dynamic_update_index_in_dim)/dynamic_update_slice | solution.py:103
  77.5 1.5 %bitcast_dynamic-update-slice_fusion.16 = (f32[8,64,128]{2,1,0:T(8,128)}, f32[64,128]{1,0:T(8,128)S(1)}, f32[8,64,128]{2,1,0:T(8,128)}, f32[8,64,128]{2,1,0:T(8,...) fusion(f32[8,64,128]{2,1,0:T(8,128)} %get-tuple-element.1309, s32[]{:T(128)S(6)} %copy.408, ...), kind=kLoop, calls=%fused_computation.clone.1 | loop fusion | flops 122880 | bytes 458757 | tf_op jit(solution)/shard_map/while/body/jit(dynamic_update_index_in_dim)/dynamic_update_slice | solution.py:103
  79.0 1.5 %bitcast_dynamic-update-slice_fusion.16 = (f32[8,64,128]{2,1,0:T(8,128)}, f32[64,128]{1,0:T(8,128)S(1)}, f32[8,64,128]{2,1,0:T(8,128)}, f32[8,64,128]{2,1,0:T(8,...) fusion(f32[8,64,128]{2,1,0:T(8,128)} %get-tuple-element.1309, s32[]{:T(128)S(6)} %copy.408, ...), kind=kLoop, calls=%fused_computation.clone.1 | loop fusion | flops 122880 | bytes 458757 | tf_op jit(solution)/shard_map/while/body/jit(dynamic_update_index_in_dim)/dynamic_update_slice | solution.py:103
  80.5 1.5 %bitcast_dynamic-update-slice_fusion.16 = (f32[8,64,128]{2,1,0:T(8,128)}, f32[64,128]{1,0:T(8,128)S(1)}, f32[8,64,128]{2,1,0:T(8,128)}, f32[8,64,128]{2,1,0:T(8,...) fusion(f32[8,64,128]{2,1,0:T(8,128)} %get-tuple-element.1309, s32[]{:T(128)S(6)} %copy.408, ...), kind=kLoop, calls=%fused_computation.clone.1 | loop fusion | flops 122880 | bytes 458757 | tf_op jit(solution)/shard_map/while/body/jit(dynamic_update_index_in_dim)/dynamic_update_slice | solution.py:103
  82.0 1.5 %bitcast_dynamic-update-slice_fusion.16 = (f32[8,64,128]{2,1,0:T(8,128)}, f32[64,128]{1,0:T(8,128)S(1)}, f32[8,64,128]{2,1,0:T(8,128)}, f32[8,64,128]{2,1,0:T(8,...) fusion(f32[8,64,128]{2,1,0:T(8,128)} %get-tuple-element.1309, s32[]{:T(128)S(6)} %copy.408, ...), kind=kLoop, calls=%fused_computation.clone.1 | loop fusion | flops 122880 | bytes 458757 | tf_op jit(solution)/shard_map/while/body/jit(dynamic_update_index_in_dim)/dynamic_update_slice | solution.py:103
  83.5 1.5 %bitcast_dynamic-update-slice_fusion.16 = (f32[8,64,128]{2,1,0:T(8,128)}, f32[64,128]{1,0:T(8,128)S(1)}, f32[8,64,128]{2,1,0:T(8,128)}, f32[8,64,128]{2,1,0:T(8,...) fusion(f32[8,64,128]{2,1,0:T(8,128)} %get-tuple-element.1309, s32[]{:T(128)S(6)} %copy.408, ...), kind=kLoop, calls=%fused_computation.clone.1 | loop fusion | flops 122880 | bytes 458757 | tf_op jit(solution)/shard_map/while/body/jit(dynamic_update_index_in_dim)/dynamic_update_slice | solution.py:103
  85.0 1.5 %bitcast_dynamic-update-slice_fusion.16 = (f32[8,64,128]{2,1,0:T(8,128)}, f32[64,128]{1,0:T(8,128)S(1)}, f32[8,64,128]{2,1,0:T(8,128)}, f32[8,64,128]{2,1,0:T(8,...) fusion(f32[8,64,128]{2,1,0:T(8,128)} %get-tuple-element.1309, s32[]{:T(128)S(6)} %copy.408, ...), kind=kLoop, calls=%fused_computation.clone.1 | loop fusion | flops 122880 | bytes 458757 | tf_op jit(solution)/shard_map/while/body/jit(dynamic_update_index_in_dim)/dynamic_update_slice | solution.py:103
  87.9 11.6 %while.81 = (s32[]{:T(128)}, f32[64,128]{1,0:T(8,128)S(1)}, f32[8,64,128]{2,1,0:T(8,128)}, f32[8,64,128]{2,1,0:T(8,128)}, f32[8,64,128]{2,1,0:T(8,128)}, /*index...) while((s32[]{:T(128)}, f32[64,128]{1,0:T(8,128)S(1)}, ...), condition=%wide.region_3.4_spmd.clone, body=%wide.region_2.3_spmd.clone.sunk | while | flops 40964 | bytes 262287 | solution.py:111
  87.9 1.5 %bitcast_dynamic-update-slice_fusion.17 = (f32[8,64,128]{2,1,0:T(8,128)}, f32[64,128]{1,0:T(8,128)S(1)}, f32[8,64,128]{2,1,0:T(8,128)}) fusion(f32[8,64,128]{2,1,0:T(8,128)} %get-tuple-element.1346, s32[]{:T(128)S(6)} %sub.273, f32[64,128]{1,0:T(8,128)S(1)} %get-tuple-element.1345, pred[]{:T(512)S(6)} %compare.143, ...), kind=kLoop, calls=%fused_computation.18.clone.1 | loop fusion | flops 40960 | bytes 262149 | tf_op jit(solution)/shard_map/while/body/jit(dynamic_update_index_in_dim)/dynamic_update_slice | solution.py:103
  90.8 1.5 %bitcast_dynamic-update-slice_fusion.17 = (f32[8,64,128]{2,1,0:T(8,128)}, f32[64,128]{1,0:T(8,128)S(1)}, f32[8,64,128]{2,1,0:T(8,128)}) fusion(f32[8,64,128]{2,1,0:T(8,128)} %get-tuple-element.1346, s32[]{:T(128)S(6)} %sub.273, f32[64,128]{1,0:T(8,128)S(1)} %get-tuple-element.1345, pred[]{:T(512)S(6)} %compare.143, ...), kind=kLoop, calls=%fused_computation.18.clone.1 | loop fusion | flops 40960 | bytes 262149 | tf_op jit(solution)/shard_map/while/body/jit(dynamic_update_index_in_dim)/dynamic_update_slice | solution.py:103
  92.3 1.4 %bitcast_dynamic-update-slice_fusion.17 = (f32[8,64,128]{2,1,0:T(8,128)}, f32[64,128]{1,0:T(8,128)S(1)}, f32[8,64,128]{2,1,0:T(8,128)}) fusion(f32[8,64,128]{2,1,0:T(8,128)} %get-tuple-element.1346, s32[]{:T(128)S(6)} %sub.273, f32[64,128]{1,0:T(8,128)S(1)} %get-tuple-element.1345, pred[]{:T(512)S(6)} %compare.143, ...), kind=kLoop, calls=%fused_computation.18.clone.1 | loop fusion | flops 40960 | bytes 262149 | tf_op jit(solution)/shard_map/while/body/jit(dynamic_update_index_in_dim)/dynamic_update_slice | solution.py:103
  93.7 1.4 %bitcast_dynamic-update-slice_fusion.17 = (f32[8,64,128]{2,1,0:T(8,128)}, f32[64,128]{1,0:T(8,128)S(1)}, f32[8,64,128]{2,1,0:T(8,128)}) fusion(f32[8,64,128]{2,1,0:T(8,128)} %get-tuple-element.1346, s32[]{:T(128)S(6)} %sub.273, f32[64,128]{1,0:T(8,128)S(1)} %get-tuple-element.1345, pred[]{:T(512)S(6)} %compare.143, ...), kind=kLoop, calls=%fused_computation.18.clone.1 | loop fusion | flops 40960 | bytes 262149 | tf_op jit(solution)/shard_map/while/body/jit(dynamic_update_index_in_dim)/dynamic_update_slice | solution.py:103
  95.2 1.5 %bitcast_dynamic-update-slice_fusion.17 = (f32[8,64,128]{2,1,0:T(8,128)}, f32[64,128]{1,0:T(8,128)S(1)}, f32[8,64,128]{2,1,0:T(8,128)}) fusion(f32[8,64,128]{2,1,0:T(8,128)} %get-tuple-element.1346, s32[]{:T(128)S(6)} %sub.273, f32[64,128]{1,0:T(8,128)S(1)} %get-tuple-element.1345, pred[]{:T(512)S(6)} %compare.143, ...), kind=kLoop, calls=%fused_computation.18.clone.1 | loop fusion | flops 40960 | bytes 262149 | tf_op jit(solution)/shard_map/while/body/jit(dynamic_update_index_in_dim)/dynamic_update_slice | solution.py:103
  96.6 1.4 %bitcast_dynamic-update-slice_fusion.17 = (f32[8,64,128]{2,1,0:T(8,128)}, f32[64,128]{1,0:T(8,128)S(1)}, f32[8,64,128]{2,1,0:T(8,128)}) fusion(f32[8,64,128]{2,1,0:T(8,128)} %get-tuple-element.1346, s32[]{:T(128)S(6)} %sub.273, f32[64,128]{1,0:T(8,128)S(1)} %get-tuple-element.1345, pred[]{:T(512)S(6)} %compare.143, ...), kind=kLoop, calls=%fused_computation.18.clone.1 | loop fusion | flops 40960 | bytes 262149 | tf_op jit(solution)/shard_map/while/body/jit(dynamic_update_index_in_dim)/dynamic_update_slice | solution.py:103
  98.1 1.5 %bitcast_dynamic-update-slice_fusion.17 = (f32[8,64,128]{2,1,0:T(8,128)}, f32[64,128]{1,0:T(8,128)S(1)}, f32[8,64,128]{2,1,0:T(8,128)}) fusion(f32[8,64,128]{2,1,0:T(8,128)} %get-tuple-element.1346, s32[]{:T(128)S(6)} %sub.273, f32[64,128]{1,0:T(8,128)S(1)} %get-tuple-element.1345, pred[]{:T(512)S(6)} %compare.143, ...), kind=kLoop, calls=%fused_computation.18.clone.1 | loop fusion | flops 40960 | bytes 262149 | tf_op jit(solution)/shard_map/while/body/jit(dynamic_update_index_in_dim)/dynamic_update_slice | solution.py:103
  103.3 2.1 %multiply_add_fusion.24 = (f32[64,16,128]{2,0,1:T(8,128)S(1)}, f32[64,16,128]{2,0,1:T(8,128)S(1)}, f32[64,16,128]{2,0,1:T(8,128)S(1)}, f32[64,16,128]{2,0,1:T(8,...) fusion(f32[64,16,128]{2,0,1:T(8,128)S(1)} %copy-done.5, ...), kind=kLoop, calls=%fused_computation.141 | loop fusion | flops 2359296 | bytes 11476992 | tf_op jit(solution)/shard_map/add | solution.py:56
  121.5 13.8 %all-gather.1 = f32[24,64,16]{1,2,0:T(8,128)S(1)} all-gather(f32[6,64,16]{1,2,0:T(8,128)S(1)} %constant_dynamic-update-slice_fusion), channel_id=3, replica_groups=mesh['row'=8,'col'=4] {'col'}, dimensions={0}, use_global_device_ids=true | all-gather | bytes 122880 | tf_op jit(solution)/shard_map/all_gather | solution.py:165
  (202 shorter events, 54.5 us)
Async XLA Ops:
  6.5 62.6 %all-gather.4.cloned.1.call-start = ((), (), s32[]{:S(2)}) async-start(), calls=%async_computation | async-start | bytes 1769472 | tf_op jit(solution)/shard_map/all_gather | solution.py:152
  9.1 4.4 %collective-permute-start.1 = (f32[2,64,1,128]{3,1,2,0:T(8,128)S(1)}, f32[2,64,1,128]{3,1,2,0:T(8,128)S(1)}, u32[]{:S(2)}, u32[]{:S(2)}) collective-permute-start(f32[2,64,1,128]{3,1,2,0:T(8,128)S(1)} %get-tuple-element.851), channel_id=1, source_target_pairs={{4,0},{8,4},{12,8},{16,12},{20,16},{24,20},{28,24},{5,1},{9,5},{13... | collective-permute-start | bytes 196616 | tf_op jit(solution)/shard_map/ppermute | solution.py:17
  10.4 3.9 %collective-permute-start = (f32[2,64,1,128]{3,1,2,0:T(8,128)S(1)}, f32[2,64,1,128]{3,1,2,0:T(8,128)S(1)}, u32[]{:S(2)}, u32[]{:S(2)}) collective-permute-start(f32[2,64,1,128]{3,1,2,0:T(8,128)S(1)} %get-tuple-element.850), channel_id=1, source_target_pairs={{0,4},{4,8},{8,12},{12,16},{16,20},{20,24},{24,28},{1,5},{5,9},{9,... | collective-permute-start | bytes 196616 | tf_op jit(solution)/shard_map/ppermute | solution.py:14
  15.9 7.9 %collective-permute-start.3 = (f32[2,64,18,1]{1,0,3,2:T(2,128)}, f32[2,64,18,1]{1,0,3,2:T(2,128)S(1)}, u32[]{:S(2)}, u32[]{:S(2)}) collective-permute-start(f32[2,64,18,1]{1,0,3,2:T(2,128)} %copy.304), channel_id=1, source_target_pairs={{1,0},{2,1},{3,2},{5,4},{6,5},{7,6},{9,8},{10,9},{11,10},{13,12},{... | collective-permute-start | bytes 27656 | tf_op jit(solution)/shard_map/ppermute | solution.py:17
  17.6 7.0 %collective-permute-start.2 = (f32[2,64,18,1]{1,0,3,2:T(2,128)S(1)}, f32[2,64,18,1]{1,0,3,2:T(2,128)}, u32[]{:S(2)}, u32[]{:S(2)}) collective-permute-start(f32[2,64,18,1]{1,0,3,2:T(2,128)S(1)} %copy.303), channel_id=1, source_target_pairs={{0,1},{1,2},{2,3},{4,5},{5,6},{6,7},{8,9},{9,10},{10,11},{12,13},{... | collective-permute-start | bytes 27656 | tf_op jit(solution)/shard_map/ppermute | solution.py:14
  26.8 1.0 copy-start
  26.8 1.2 copy-start.19
  26.8 1.3 copy-start.20
  36.0 1.0 copy-start.10
  38.0 1.0 copy-start.1
  39.8 4.5 %copy-start.2 = (f32[64,16,128]{2,0,1:T(8,128)}, f32[64,16,128]{2,0,1:T(8,128)S(1)}, u32[]{:S(2)}) copy-start(f32[64,16,128]{2,0,1:T(8,128)S(1)} %get-tuple-element.745) | copy-start | bytes 1572868
  39.8 4.5 %copy-start.4 = (f32[64,16,128]{2,0,1:T(8,128)}, f32[64,16,128]{2,0,1:T(8,128)S(1)}, u32[]{:S(2)}) copy-start(f32[64,16,128]{2,0,1:T(8,128)S(1)} %get-tuple-element.747) | copy-start | bytes 1572868
  73.7 27.4 %copy-start.11 = (f32[64,16,128]{2,0,1:T(8,128)S(1)}, f32[64,16,128]{2,0,1:T(8,128)}, u32[]{:S(2)}) copy-start(f32[64,16,128]{2,0,1:T(8,128)} %copy-done.10) | copy-start | bytes 1572868
  74.4 26.7 %copy-start.9 = (f32[64,16,128]{2,0,1:T(8,128)S(1)}, f32[64,16,128]{2,0,1:T(8,128)}, u32[]{:S(2)}) copy-start(f32[64,16,128]{2,0,1:T(8,128)} %copy-done.8) | copy-start | bytes 1572868
  86.5 14.6 %copy-start.7 = (f32[64,16,128]{2,0,1:T(8,128)S(1)}, f32[64,16,128]{2,0,1:T(8,128)}, u32[]{:S(2)}) copy-start(f32[64,16,128]{2,0,1:T(8,128)} %copy-done.6) | copy-start | bytes 1572868
  101.1 1.0 copy-start.15
  101.1 1.2 copy-start.16
  101.1 1.3 copy-start.17
  101.1 1.5 %copy-start.18 = (f32[64,16,127]{2,0,1:T(8,128)S(1)}, f32[64,16,127]{2,0,1:T(8,128)}, u32[]{:S(2)}) copy-start(f32[64,16,127]{2,0,1:T(8,128)} %get-tuple-element.972) | copy-start | bytes 1560580
  101.2 1.5 %copy-start.3 = (f32[64,16,128]{2,0,1:T(8,128)S(1)}, f32[64,16,128]{2,0,1:T(8,128)}, u32[]{:S(2)}) copy-start(f32[64,16,128]{2,0,1:T(8,128)} %copy-done.2) | copy-start | bytes 1572868
  101.2 1.7 %copy-start.5 = (f32[64,16,128]{2,0,1:T(8,128)S(1)}, f32[64,16,128]{2,0,1:T(8,128)}, u32[]{:S(2)}) copy-start(f32[64,16,128]{2,0,1:T(8,128)} %copy-done.4) | copy-start | bytes 1572868
  101.3 1.8 %copy-start.13 = (f32[64,16,127]{2,0,1:T(8,128)S(1)}, f32[64,16,127]{2,0,1:T(8,128)}, u32[]{:S(2)}) copy-start(f32[64,16,127]{2,0,1:T(8,128)} %get-tuple-element.938) | copy-start | bytes 1560580
  101.3 2.0 %copy-start.14 = (f32[64,16,127]{2,0,1:T(8,128)S(1)}, f32[64,16,127]{2,0,1:T(8,128)}, u32[]{:S(2)}) copy-start(f32[64,16,127]{2,0,1:T(8,128)} %get-tuple-element.939) | copy-start | bytes 1560580
  121.5 14.4 %copy-start.12 = (f32[64,16,128]{2,1,0:T(8,128)S(1)}, f32[64,16,128]{2,1,0:T(8,128)}, u32[]{:S(2)}) copy-start(f32[64,16,128]{2,1,0:T(8,128)} %param.10) | copy-start | bytes 1572868
  (3 other events, 2.3 us)
Sparse Core Ops, SparseCore 0:
  37.9 31.1 all-gather.3
where the time goes:
time: 146 us; the launch traced here: 144 us
  other arithmetic  43.1 us (30%)
  local copies, waits for them, and re-layouts  36.4 us (25%)
  waiting for transfers between devices  24.6 us (17%)
  between operations  14.2 us (10%)
  blocking collectives  13.8 us (9%)
  starting transfers between devices  11.8 us (8%)
    dynamic_update_slice x24, other arithmetic, join_spikes(): unused, outputs = lax.scan(forward, (zero_plane, zero_plane), columns_in)  23.8 us
    all_gather x1, waiting for transfers between devices, on_device(): gathered = lax.all_gather(planes, 'row', axis=0, tiled=True)  23.3 us
    all_gather x1, blocking collectives, on_device(): gathered = lax.all_gather(planes, 'col', axis=0, tiled=True)  13.8 us
    add x11, other arithmetic, reduce_lines(): column + left_factor * shifted(column, line_axis, stride, 0.0)  10.7 us
    slice x41, local copies, waits for them, and re-layouts, shifted(): kept_part = lax.slice_in_dim(values, 0, length - stride, axis=line_axis)  9.44 us
    ppermute x2, starting transfers between devices, padded_2(): lax.ppermute(lax.slice_in_dim(block, block.shape[dim] - width, None, axis...  9.22 us
    unnamed x55, local copies, waits for them, and re-layouts  8.25 us
    slice x24, local copies, waits for them, and re-layouts, shifted(): kept_part = lax.slice_in_dim(values, -stride, length, axis=line_axis)  5.6 us
  transfers between devices with their start and end apart: 5, of which 3 were waited for; matrix products, arithmetic and copies ran while one was open for 6% of the time, Pallas kernels for 0%

commit v1 on v0

--- a/solution.py
+++ b/solution.py
@@ -149,7 +149,14 @@
     )
     explicit = flux_xdir + flux_ydir + flux_zdir
     local_part, left_spike, right_spike, planes = local_spikes(-west_xdir, -east_xdir, explicit, 1)
-    gathered = lax.all_gather(planes, "row", axis=0, tiled=True)
+    size = lax.axis_size("row")
+    hops = [(i_2, (i_2 + 1) % size) for i_2 in range(size)]
+    parts = [planes]
+    for far in range(1, size):
+        parts = [lax.ppermute(parts[0], "row", hops), *parts]
+    whole = jnp.concatenate(parts, axis=0)
+    turn = (lax.axis_index("row") + 1) * parts[-1].shape[0]
+    gathered = jnp.roll(whole, turn, axis=0)
     delta_xdir = join_spikes(
         gathered,
         local_part,

time: 146 us -> 143 us (0.979)
  the two profiles are of different devices: /device:TPU:0 before, /device:TPU:4 now
where the time goes in v1:
time: 143 us; the launch traced here: 142 us
  other arithmetic  44.7 us (31%)
  waiting for transfers between devices  38.7 us (27%)
  local copies, waits for them, and re-layouts  31.2 us (22%)
  blocking collectives  14.8 us (10%)
  starting transfers between devices  11.2 us (8%)
    ppermute x7, waiting for transfers between devices, on_device(): parts = [lax.ppermute(parts[0], 'row', hops), *parts]  34.7 us
    dynamic_update_slice x24, other arithmetic, join_spikes(): unused, outputs = lax.scan(forward, (zero_plane, zero_plane), columns_in)  23.6 us
    all_gather x1, blocking collectives, on_device(): gathered = lax.all_gather(planes, 'col', axis=0, tiled=True)  14.8 us
    add x11, other arithmetic, reduce_lines(): column + left_factor * shifted(column, line_axis, stride, 0.0)  9.65 us
    slice x41, local copies, waits for them, and re-layouts, shifted(): kept_part = lax.slice_in_dim(values, 0, length - stride, axis=line_axis)  9.16 us
    ppermute x2, starting transfers between devices, padded_2(): lax.ppermute(lax.slice_in_dim(block, block.shape[dim] - width, None, axis...  7.07 us
    unnamed x64, local copies, waits for them, and re-layouts  5.92 us
    slice x24, local copies, waits for them, and re-layouts, shifted(): kept_part = lax.slice_in_dim(values, -stride, length, axis=line_axis)  5.56 us
  transfers between devices with their start and end apart: 11, of which 8 were waited for; matrix products, arithmetic and copies ran while one was open for 6% of the time, Pallas kernels for 0%

profile of v1, /device:TPU:4, one launch (start us, length us, event | category | flops | bytes accessed | tf_op | source)
XLA Modules:
  0.0 141.8 jit_solution(13421077320948822271)
XLA Ops:
  0.0 2.5 %fusion.53 = (f32[64,16,128]{2,0,1:T(8,128)}, f32[1,64,16,128]{3,1,2,0:T(8,128)S(1)}, f32[1,64,16,128]{3,1,2,0:T(8,128)S(1)}, f32[64,16,128]{2,0,1:T(8,128)}) fusion(f32[64,16,128]{2,1,0:T(8,128)} %param.10, f32[64,16,128]{2,1,0:T(8,128)} %param.11), kind=kLoop, calls=%fused_computation.257 | loop fusion | bytes 3145728 | tf_op args[0]
  2.5 2.8 %collective-permute-start.1 = (f32[2,64,1,128]{3,1,2,0:T(8,128)S(1)}, f32[2,64,1,128]{3,1,2,0:T(8,128)S(1)}, u32[]{:S(2)}, u32[]{:S(2)}) collective-permute-start(f32[2,64,1,128]{3,1,2,0:T(8,128)S(1)} %get-tuple-element.864), channel_id=1, source_target_pairs={{4,0},{8,4},{12,8},{16,12},{20,16},{24,20},{28,24},{5,1},{9,5},{13... | collective-permute-start | bytes 196616 | tf_op jit(solution)/shard_map/ppermute | solution.py:17
  5.3 1.9 %collective-permute-start = (f32[2,64,1,128]{3,1,2,0:T(8,128)S(1)}, f32[2,64,1,128]{3,1,2,0:T(8,128)S(1)}, u32[]{:S(2)}, u32[]{:S(2)}) collective-permute-start(f32[2,64,1,128]{3,1,2,0:T(8,128)S(1)} %get-tuple-element.863), channel_id=1, source_target_pairs={{0,4},{4,8},{8,12},{12,16},{16,20},{20,24},{24,28},{1,5},{5,9},{9,... | collective-permute-start | bytes 196616 | tf_op jit(solution)/shard_map/ppermute | solution.py:14
  7.8 4.0 %collective-permute-done = f32[2,64,1,128]{3,1,2,0:T(8,128)S(1)} collective-permute-done((f32[2,64,1,128]{3,1,2,0:T(8,128)S(1)}, f32[2,64,1,128]{3,1,2,0:T(8,128)S(1)}, u32[]{:S(2)}, u32[]{:S(2)}) %collective-permute-start) | collective-permute-done | bytes 65568 | tf_op jit(solution)/shard_map/ppermute | solution.py:14
  15.1 5.2 %collective-permute-start.2 = (f32[2,64,18,1]{1,0,3,2:T(2,128)S(1)}, f32[2,64,18,1]{1,0,3,2:T(2,128)}, u32[]{:S(2)}, u32[]{:S(2)}) collective-permute-start(f32[2,64,18,1]{1,0,3,2:T(2,128)S(1)} %copy.267), channel_id=1, source_target_pairs={{0,1},{1,2},{2,3},{4,5},{5,6},{6,7},{8,9},{9,10},{10,11},{12,13},{... | collective-permute-start | bytes 27656 | tf_op jit(solution)/shard_map/ppermute | solution.py:14
  22.5 1.9 %pad_maximum_fusion = f32[2,64,18,130]{3,1,2,0:T(8,128)S(1)} fusion(f32[2,64,18,1]{3,1,2,0:T(8,128)S(1)} %copy.270, f32[2,64,1,128]{3,1,2,0:T(8,128)} %copy-done.14, f32[1,64,16,128]{3,1,2,0:T(8,128)S(1)} %get-tuple-element.1003, f32[1,64,16,128]{3,1,2,0:T(8,128)S(1)} %get-tuple-element.896, f32[2,64,1,128]{3,1,2,0:T(8,128)} %copy-done.15, ...), kind=kLoop, calls=%fused_computation.42 | loop fusion | flops 1497600 | bytes 2396160 | tf_op jit(solution)/shard_map/concatenate | solution.py:18
  36.1 4.5 %collective-permute-done.4 = f32[1,6,64,128]{3,2,1,0:T(8,128)S(1)} collective-permute-done((f32[1,6,64,128]{3,2,1,0:T(8,128)S(1)}, f32[1,6,64,128]{3,2,1,0:T(8,128)S(1)}, u32[]{:S(2)}, u32[]{:S(2)}) %collective-permute-start.4) | collective-permute-done | bytes 196640 | tf_op jit(solution)/shard_map/ppermute | solution.py:156
  41.5 5.0 %collective-permute-done.5 = f32[1,6,64,128]{3,2,1,0:T(8,128)S(1)} collective-permute-done((f32[1,6,64,128]{3,2,1,0:T(8,128)S(1)}, f32[1,6,64,128]{3,2,1,0:T(8,128)S(1)}, u32[]{:S(2)}, u32[]{:S(2)}) %collective-permute-start.5) | collective-permute-done | bytes 196640 | tf_op jit(solution)/shard_map/ppermute | solution.py:156
  47.6 5.0 %collective-permute-done.6 = f32[1,6,64,128]{3,2,1,0:T(8,128)S(1)} collective-permute-done((f32[1,6,64,128]{3,2,1,0:T(8,128)S(1)}, f32[1,6,64,128]{3,2,1,0:T(8,128)S(1)}, u32[]{:S(2)}, u32[]{:S(2)}) %collective-permute-start.6) | collective-permute-done | bytes 196640 | tf_op jit(solution)/shard_map/ppermute | solution.py:156
  52.8 5.7 %collective-permute-done.7 = f32[1,6,64,128]{3,2,1,0:T(8,128)S(1)} collective-permute-done((f32[1,6,64,128]{3,2,1,0:T(8,128)S(1)}, f32[1,6,64,128]{3,2,1,0:T(8,128)S(1)}, u32[]{:S(2)}, u32[]{:S(2)}) %collective-permute-start.7) | collective-permute-done | bytes 196640 | tf_op jit(solution)/shard_map/ppermute | solution.py:156
  59.7 4.9 %collective-permute-done.8 = f32[1,6,64,128]{3,2,1,0:T(8,128)S(1)} collective-permute-done((f32[1,6,64,128]{3,2,1,0:T(8,128)S(1)}, f32[1,6,64,128]{3,2,1,0:T(8,128)S(1)}, u32[]{:S(2)}, u32[]{:S(2)}) %collective-permute-start.8) | collective-permute-done | bytes 196640 | tf_op jit(solution)/shard_map/ppermute | solution.py:156
  65.7 4.8 %collective-permute-done.9 = f32[1,6,64,128]{3,2,1,0:T(8,128)S(1)} collective-permute-done((f32[1,6,64,128]{3,2,1,0:T(8,128)S(1)}, f32[1,6,64,128]{3,2,1,0:T(8,128)S(1)}, u32[]{:S(2)}, u32[]{:S(2)}) %collective-permute-start.9) | collective-permute-done | bytes 196640 | tf_op jit(solution)/shard_map/ppermute | solution.py:156
  71.7 4.8 %collective-permute-done.10 = f32[1,6,64,128]{3,2,1,0:T(8,128)S(1)} collective-permute-done((f32[1,6,64,128]{3,2,1,0:T(8,128)S(1)}, f32[1,6,64,128]{3,2,1,0:T(8,128)S(1)}, u32[]{:S(2)}, u32[]{:S(2)}) %collective-permute-start.10) | collective-permute-done | bytes 196640 | tf_op jit(solution)/shard_map/ppermute | solution.py:156
  80.9 12.0 %while.80 = (s32[]{:T(128)}, f32[64,128]{1,0:T(8,128)S(1)}, f32[64,128]{1,0:T(8,128)S(1)}, f32[8,64,128]{2,1,0:T(8,128)}, f32[8,64,128]{2,1,0:T(8,128)}, /*index...) while((s32[]{:T(128)}, f32[64,128]{1,0:T(8,128)S(1)}, ...), condition=%wide.region_1.2_spmd.clone, body=%wide.region_0.1_spmd.clone.sunk | while | flops 122883 | bytes 458915 | solution.py:103
  80.9 1.5 %bitcast_dynamic-update-slice_fusion.16 = (f32[8,64,128]{2,1,0:T(8,128)}, f32[64,128]{1,0:T(8,128)S(1)}, f32[8,64,128]{2,1,0:T(8,128)}, f32[8,64,128]{2,1,0:T(8,...) fusion(f32[8,64,128]{2,1,0:T(8,128)} %get-tuple-element.1322, s32[]{:T(128)S(6)} %copy.375, ...), kind=kLoop, calls=%fused_computation.clone.1 | loop fusion | flops 122880 | bytes 458757 | tf_op jit(solution)/shard_map/while/body/jit(dynamic_update_index_in_dim)/dynamic_update_slice | solution.py:103
  82.4 1.5 %bitcast_dynamic-update-slice_fusion.16 = (f32[8,64,128]{2,1,0:T(8,128)}, f32[64,128]{1,0:T(8,128)S(1)}, f32[8,64,128]{2,1,0:T(8,128)}, f32[8,64,128]{2,1,0:T(8,...) fusion(f32[8,64,128]{2,1,0:T(8,128)} %get-tuple-element.1322, s32[]{:T(128)S(6)} %copy.375, ...), kind=kLoop, calls=%fused_computation.clone.1 | loop fusion | flops 122880 | bytes 458757 | tf_op jit(solution)/shard_map/while/body/jit(dynamic_update_index_in_dim)/dynamic_update_slice | solution.py:103
  83.9 1.5 %bitcast_dynamic-update-slice_fusion.16 = (f32[8,64,128]{2,1,0:T(8,128)}, f32[64,128]{1,0:T(8,128)S(1)}, f32[8,64,128]{2,1,0:T(8,128)}, f32[8,64,128]{2,1,0:T(8,...) fusion(f32[8,64,128]{2,1,0:T(8,128)} %get-tuple-element.1322, s32[]{:T(128)S(6)} %copy.375, ...), kind=kLoop, calls=%fused_computation.clone.1 | loop fusion | flops 122880 | bytes 458757 | tf_op jit(solution)/shard_map/while/body/jit(dynamic_update_index_in_dim)/dynamic_update_slice | solution.py:103
  85.4 1.5 %bitcast_dynamic-update-slice_fusion.16 = (f32[8,64,128]{2,1,0:T(8,128)}, f32[64,128]{1,0:T(8,128)S(1)}, f32[8,64,128]{2,1,0:T(8,128)}, f32[8,64,128]{2,1,0:T(8,...) fusion(f32[8,64,128]{2,1,0:T(8,128)} %get-tuple-element.1322, s32[]{:T(128)S(6)} %copy.375, ...), kind=kLoop, calls=%fused_computation.clone.1 | loop fusion | flops 122880 | bytes 458757 | tf_op jit(solution)/shard_map/while/body/jit(dynamic_update_index_in_dim)/dynamic_update_slice | solution.py:103
  88.4 1.5 %bitcast_dynamic-update-slice_fusion.16 = (f32[8,64,128]{2,1,0:T(8,128)}, f32[64,128]{1,0:T(8,128)S(1)}, f32[8,64,128]{2,1,0:T(8,128)}, f32[8,64,128]{2,1,0:T(8,...) fusion(f32[8,64,128]{2,1,0:T(8,128)} %get-tuple-element.1322, s32[]{:T(128)S(6)} %copy.375, ...), kind=kLoop, calls=%fused_computation.clone.1 | loop fusion | flops 122880 | bytes 458757 | tf_op jit(solution)/shard_map/while/body/jit(dynamic_update_index_in_dim)/dynamic_update_slice | solution.py:103
  89.9 1.5 %bitcast_dynamic-update-slice_fusion.16 = (f32[8,64,128]{2,1,0:T(8,128)}, f32[64,128]{1,0:T(8,128)S(1)}, f32[8,64,128]{2,1,0:T(8,128)}, f32[8,64,128]{2,1,0:T(8,...) fusion(f32[8,64,128]{2,1,0:T(8,128)} %get-tuple-element.1322, s32[]{:T(128)S(6)} %copy.375, ...), kind=kLoop, calls=%fused_computation.clone.1 | loop fusion | flops 122880 | bytes 458757 | tf_op jit(solution)/shard_map/while/body/jit(dynamic_update_index_in_dim)/dynamic_update_slice | solution.py:103
  91.4 1.5 %bitcast_dynamic-update-slice_fusion.16 = (f32[8,64,128]{2,1,0:T(8,128)}, f32[64,128]{1,0:T(8,128)S(1)}, f32[8,64,128]{2,1,0:T(8,128)}, f32[8,64,128]{2,1,0:T(8,...) fusion(f32[8,64,128]{2,1,0:T(8,128)} %get-tuple-element.1322, s32[]{:T(128)S(6)} %copy.375, ...), kind=kLoop, calls=%fused_computation.clone.1 | loop fusion | flops 122880 | bytes 458757 | tf_op jit(solution)/shard_map/while/body/jit(dynamic_update_index_in_dim)/dynamic_update_slice | solution.py:103
  93.7 11.4 %while.81 = (s32[]{:T(128)}, f32[64,128]{1,0:T(8,128)S(1)}, f32[8,64,128]{2,1,0:T(8,128)S(1)}, f32[8,64,128]{2,1,0:T(8,128)}, f32[8,64,128]{2,1,0:T(8,128)}, /*i...) while((s32[]{:T(128)}, f32[64,128]{1,0:T(8,128)S(1)}, ...), condition=%wide.region_3.4_spmd.clone, body=%wide.region_2.3_spmd.clone.sunk | while | flops 40964 | bytes 262287 | solution.py:111
  106.1 1.6 %multiply_subtract_fusion = f32[64,16,128]{2,0,1:T(8,128)S(1)} fusion(f32[64,16,128]{2,0,1:T(8,128)} %copy-done.2, f32[64,16,128]{2,0,1:T(8,128)S(1)} %add_divide_fusion.5, f32[64,16,128]{2,0,1:T(8,128)} %copy-done.1, f32[64,128]{1,0:T(8,128)S(1)} %multiply_bitcast_fusion, f32[64,128]{1,0:T(8,128)S(1)} %multiply_bitcast_fusion.1), kind=kLoop, calls=%fused_computation.145 | loop fusion | flops 524288 | bytes 2162688 | tf_op jit(solution)/shard_map/sub | solution.py:120
  125.0 14.8 %all-gather = f32[24,64,16]{1,2,0:T(8,128)S(1)} all-gather(f32[6,64,16]{1,2,0:T(8,128)S(1)} %constant_dynamic-update-slice_fusion.22), channel_id=2, replica_groups=mesh['row'=8,'col'=4] {'col'}, dimensions={0}, use_global_device_ids=true | all-gather | bytes 122880 | tf_op jit(solution)/shard_map/all_gather | solution.py:172
  (223 shorter events, 61.1 us)
Async XLA Ops:
  2.5 5.3 %collective-permute-start.1 = (f32[2,64,1,128]{3,1,2,0:T(8,128)S(1)}, f32[2,64,1,128]{3,1,2,0:T(8,128)S(1)}, u32[]{:S(2)}, u32[]{:S(2)}) collective-permute-start(f32[2,64,1,128]{3,1,2,0:T(8,128)S(1)} %get-tuple-element.864), channel_id=1, source_target_pairs={{4,0},{8,4},{12,8},{16,12},{20,16},{24,20},{28,24},{5,1},{9,5},{13... | collective-permute-start | bytes 196616 | tf_op jit(solution)/shard_map/ppermute | solution.py:17
  5.3 6.5 %collective-permute-start = (f32[2,64,1,128]{3,1,2,0:T(8,128)S(1)}, f32[2,64,1,128]{3,1,2,0:T(8,128)S(1)}, u32[]{:S(2)}, u32[]{:S(2)}) collective-permute-start(f32[2,64,1,128]{3,1,2,0:T(8,128)S(1)} %get-tuple-element.863), channel_id=1, source_target_pairs={{0,4},{4,8},{8,12},{12,16},{16,20},{20,24},{24,28},{1,5},{5,9},{9,... | collective-permute-start | bytes 196616 | tf_op jit(solution)/shard_map/ppermute | solution.py:14
  7.8 4.0 %copy-start.14 = (f32[2,64,1,128]{3,1,2,0:T(8,128)}, f32[2,64,1,128]{3,1,2,0:T(8,128)S(1)}, u32[]{:S(2)}) copy-start(f32[2,64,1,128]{3,1,2,0:T(8,128)S(1)} %collective-permute-done.1) | copy-start | bytes 196612
  13.4 7.4 %collective-permute-start.3 = (f32[2,64,18,1]{1,0,3,2:T(2,128)S(1)}, f32[2,64,18,1]{1,0,3,2:T(2,128)S(1)}, u32[]{:S(2)}, u32[]{:S(2)}) collective-permute-start(f32[2,64,18,1]{1,0,3,2:T(2,128)S(1)} %copy.268), channel_id=1, source_target_pairs={{1,0},{2,1},{3,2},{5,4},{6,5},{7,6},{9,8},{10,9},{11,10},{13,12},{... | collective-permute-start | bytes 27656 | tf_op jit(solution)/shard_map/ppermute | solution.py:17
  15.1 6.2 %collective-permute-start.2 = (f32[2,64,18,1]{1,0,3,2:T(2,128)S(1)}, f32[2,64,18,1]{1,0,3,2:T(2,128)}, u32[]{:S(2)}, u32[]{:S(2)}) collective-permute-start(f32[2,64,18,1]{1,0,3,2:T(2,128)S(1)} %copy.267), channel_id=1, source_target_pairs={{0,1},{1,2},{2,3},{4,5},{5,6},{6,7},{8,9},{9,10},{10,11},{12,13},{... | collective-permute-start | bytes 27656 | tf_op jit(solution)/shard_map/ppermute | solution.py:14
  24.3 1.3 copy-start.13
  24.4 1.3 copy-start.16
  33.8 1.5 %copy-start.17 = (pred[128]{0:T(512)(128)(4,1)S(1)}, pred[128]{0:T(512)(128)(4,1)}, u32[]{:S(2)}) copy-start(pred[128]{0:T(512)(128)(4,1)} %get-tuple-element.1007) | copy-start | bytes 388
  34.5 6.0 %collective-permute-start.4 = (f32[1,6,64,128]{3,2,1,0:T(8,128)S(1)}, f32[1,6,64,128]{3,2,1,0:T(8,128)S(1)}, u32[]{:S(2)}, u32[]{:S(2)}) collective-permute-start(f32[1,6,64,128]{3,2,1,0:T(8,128)S(1)} %bitcast.271), channel_id=1, source_target_pairs={{0,4},{4,8},{8,12},{12,16},{16,20},{20,24},{24,28},{28,0},{1,5},{5... | collective-permute-start | bytes 589832 | tf_op jit(solution)/shard_map/ppermute | solution.py:156
  40.5 6.0 %collective-permute-start.5 = (f32[1,6,64,128]{3,2,1,0:T(8,128)S(1)}, f32[1,6,64,128]{3,2,1,0:T(8,128)S(1)}, u32[]{:S(2)}, u32[]{:S(2)}) collective-permute-start(f32[1,6,64,128]{3,2,1,0:T(8,128)S(1)} %collective-permute-done.4), channel_id=1, source_target_pairs={{0,4},{4,8},{8,12},{12,16},{16,20},{20,24},{24,28},{28,0},{1,5},{5... | collective-permute-start | bytes 589832 | tf_op jit(solution)/shard_map/ppermute | solution.py:156
  46.5 6.0 %collective-permute-start.6 = (f32[1,6,64,128]{3,2,1,0:T(8,128)S(1)}, f32[1,6,64,128]{3,2,1,0:T(8,128)S(1)}, u32[]{:S(2)}, u32[]{:S(2)}) collective-permute-start(f32[1,6,64,128]{3,2,1,0:T(8,128)S(1)} %collective-permute-done.5), channel_id=1, source_target_pairs={{0,4},{4,8},{8,12},{12,16},{16,20},{20,24},{24,28},{28,0},{1,5},{5... | collective-permute-start | bytes 589832 | tf_op jit(solution)/shard_map/ppermute | solution.py:156
  52.5 6.0 %collective-permute-start.7 = (f32[1,6,64,128]{3,2,1,0:T(8,128)S(1)}, f32[1,6,64,128]{3,2,1,0:T(8,128)S(1)}, u32[]{:S(2)}, u32[]{:S(2)}) collective-permute-start(f32[1,6,64,128]{3,2,1,0:T(8,128)S(1)} %collective-permute-done.6), channel_id=1, source_target_pairs={{0,4},{4,8},{8,12},{12,16},{16,20},{20,24},{24,28},{28,0},{1,5},{5... | collective-permute-start | bytes 589832 | tf_op jit(solution)/shard_map/ppermute | solution.py:156
  58.5 6.0 %collective-permute-start.8 = (f32[1,6,64,128]{3,2,1,0:T(8,128)S(1)}, f32[1,6,64,128]{3,2,1,0:T(8,128)S(1)}, u32[]{:S(2)}, u32[]{:S(2)}) collective-permute-start(f32[1,6,64,128]{3,2,1,0:T(8,128)S(1)} %collective-permute-done.7), channel_id=1, source_target_pairs={{0,4},{4,8},{8,12},{12,16},{16,20},{20,24},{24,28},{28,0},{1,5},{5... | collective-permute-start | bytes 589832 | tf_op jit(solution)/shard_map/ppermute | solution.py:156
  64.5 6.0 %collective-permute-start.9 = (f32[1,6,64,128]{3,2,1,0:T(8,128)S(1)}, f32[1,6,64,128]{3,2,1,0:T(8,128)S(1)}, u32[]{:S(2)}, u32[]{:S(2)}) collective-permute-start(f32[1,6,64,128]{3,2,1,0:T(8,128)S(1)} %collective-permute-done.8), channel_id=1, source_target_pairs={{0,4},{4,8},{8,12},{12,16},{16,20},{20,24},{24,28},{28,0},{1,5},{5... | collective-permute-start | bytes 589832 | tf_op jit(solution)/shard_map/ppermute | solution.py:156
  70.5 6.0 %collective-permute-start.10 = (f32[1,6,64,128]{3,2,1,0:T(8,128)S(1)}, f32[1,6,64,128]{3,2,1,0:T(8,128)S(1)}, u32[]{:S(2)}, u32[]{:S(2)}) collective-permute-start(f32[1,6,64,128]{3,2,1,0:T(8,128)S(1)} %collective-permute-done.9), channel_id=1, source_target_pairs={{0,4},{4,8},{8,12},{12,16},{16,20},{20,24},{24,28},{28,0},{1,5},{5... | collective-permute-start | bytes 589832 | tf_op jit(solution)/shard_map/ppermute | solution.py:156
  105.1 2.8 %copy-start.4 = (f32[64,16,127]{2,0,1:T(8,128)S(1)}, f32[64,16,127]{2,0,1:T(8,128)}, u32[]{:S(2)}) copy-start(f32[64,16,127]{2,0,1:T(8,128)} %get-tuple-element.989) | copy-start | bytes 1560580
  105.1 2.8 %copy-start.5 = (f32[64,16,127]{2,0,1:T(8,128)S(1)}, f32[64,16,127]{2,0,1:T(8,128)}, u32[]{:S(2)}) copy-start(f32[64,16,127]{2,0,1:T(8,128)} %get-tuple-element.985) | copy-start | bytes 1560580
  105.1 2.8 %copy-start.6 = (f32[64,16,127]{2,0,1:T(8,128)S(1)}, f32[64,16,127]{2,0,1:T(8,128)}, u32[]{:S(2)}) copy-start(f32[64,16,127]{2,0,1:T(8,128)} %get-tuple-element.951) | copy-start | bytes 1560580
  105.1 2.8 %copy-start.7 = (f32[64,16,127]{2,0,1:T(8,128)S(1)}, f32[64,16,127]{2,0,1:T(8,128)}, u32[]{:S(2)}) copy-start(f32[64,16,127]{2,0,1:T(8,128)} %get-tuple-element.952) | copy-start | bytes 1560580
  105.1 2.8 %copy-start.8 = (f32[64,16,126]{2,0,1:T(8,128)S(1)}, f32[64,16,126]{2,0,1:T(8,128)}, u32[]{:S(2)}) copy-start(f32[64,16,126]{2,0,1:T(8,128)} %get-tuple-element.991) | copy-start | bytes 1548292
  105.1 2.8 %copy-start.9 = (f32[64,16,126]{2,0,1:T(8,128)S(1)}, f32[64,16,126]{2,0,1:T(8,128)}, u32[]{:S(2)}) copy-start(f32[64,16,126]{2,0,1:T(8,128)} %get-tuple-element.992) | copy-start | bytes 1548292
  105.1 2.8 %copy-start.10 = (f32[64,16,126]{2,0,1:T(8,128)S(1)}, f32[64,16,126]{2,0,1:T(8,128)}, u32[]{:S(2)}) copy-start(f32[64,16,126]{2,0,1:T(8,128)} %get-tuple-element.987) | copy-start | bytes 1548292
  105.1 2.8 %copy-start.11 = (f32[64,16,126]{2,0,1:T(8,128)S(1)}, f32[64,16,126]{2,0,1:T(8,128)}, u32[]{:S(2)}) copy-start(f32[64,16,126]{2,0,1:T(8,128)} %get-tuple-element.988) | copy-start | bytes 1548292
  123.9 16.4 %copy-start.3 = (f32[64,16,128]{2,1,0:T(8,128)S(1)}, f32[64,16,128]{2,1,0:T(8,128)}, u32[]{:S(2)}) copy-start(f32[64,16,128]{2,1,0:T(8,128)} %param.10) | copy-start | bytes 1572868
  (6 other events, 5.3 us)
